TPU v7x, 32 devices: a whole 2x2x4 slice. The times are simulated.
32 devices in a mesh: section: 8 (over y, x, core), tp: 4 (over z).
Axes of the slice: x: 2, y: 2, z: 4, core: 2. Of those that a mesh axis runs over, the one named last changes fastest.
Arguments:
- tokens_in: bfloat16 [2, 224, 7168], P(None, None, 'tp'), may hold values from -6 to 6
- norm_gain: float32 [2, 7168], P(None, 'tp'), may hold values from 0.5 to 2
- router_weight: float32 [2, 7168], P(None, 'tp'), may hold values from -0.0625 to 0.0625
- gate_weight: bfloat16 [8, 7168, 4608], P('section', 'tp'), may hold values from -0.0625 to 0.0625
- up_weight: bfloat16 [8, 7168, 4608], P('section', 'tp'), may hold values from -0.0625 to 0.0625
- down_weight: bfloat16 [8, 4608, 7168], P('section', None, 'tp'), may hold values from -0.046875 to 0.046875
- routed_rows: int32 [2, 2, 112], replicated, may hold values from 0 to 223, as said below
- routed_count: int32 [2, 2], replicated, may hold values from 56 to 112, as said below
Outputs:
- tokens_out: bfloat16 [2, 224, 7168], P(None, 'section', 'tp')
Inputs may be any that keep to these rules, and one draw needn't show every extreme that they name: `routed_rows`: within each microbatch and layer, the 112 entries are distinct token positions. Only the leading routed_count entries of a list are live; some list is full in every draw.
All inputs are finite; a program needn't handle non-finite values.
Results may differ from a plain program's by a relative error of at most 0.0074.
Values may be sent and summed in bfloat16 or wider, within the bound.
No kernel may reach another device: no remote copies, remote signals or barrier semaphores. Data moves between devices by JAX's collectives and lax.ppermute only.
A program may use at most 128 MiB of HBM per device.

v0:
```python
import jax
import jax.numpy as jnp
from jax import lax
from jax.sharding import PartitionSpec as P

D = 7168
LAYERS = 2


EPSILON = 1e-06


def swapped(value, axis, distance):
    mask = 2**distance
    pairs = [(source, source ^ mask) for source in range(lax.axis_size(axis))]
    return lax.ppermute(value, axis, pairs)


def shifted(value, axis, by):
    length = lax.axis_size(axis)
    pairs = [(i, i + by) for i in range(length) if 0 <= i + by < length]
    return lax.ppermute(value, axis, pairs)


def on_device(
    tokens_in,
    norm_gain,
    router_weight,
    gate_weight,
    up_weight,
    down_weight,
    routed_rows,
    routed_count,
):
    micro_count, token_count, quarter = tokens_in.shape
    capacity = routed_rows.shape[2]
    section_index = lax.axis_index("section")
    group_size = lax.axis_size("section") // LAYERS
    bit_count = group_size.bit_length() - 1
    layer_index = section_index // group_size
    total_steps = micro_count + LAYERS - 1
    gain_row = norm_gain[layer_index]
    router_row = router_weight[layer_index]
    gate_block = gate_weight[0]
    up_block = up_weight[0]
    down_block = down_weight[0]

    def sum_groups(partial_value):
        piece = partial_value
        for bit in reversed(range(bit_count)):
            half = piece.shape[1] // 2
            upper_side = section_index // 2**bit % 2 == 1
            lower, upper = (piece[:, :half], piece[:, half:])
            keep = jnp.where(upper_side, upper, lower)
            give = jnp.where(upper_side, lower, upper)
            piece = keep + swapped(give, "section", bit)
        for bit in range(bit_count):
            upper_side = section_index // 2**bit % 2 == 1
            other = swapped(piece, "section", bit)
            piece = jnp.where(
                upper_side,
                jnp.concatenate([other, piece], axis=1),
                jnp.concatenate([piece, other], axis=1),
            )
        return piece

    def apply_layer(stream, micro_index):
        routed_ids = routed_rows[micro_index, layer_index]
        live_count = routed_count[micro_index, layer_index]
        picked = jnp.take(stream, routed_ids, axis=0)
        floats = picked.astype(jnp.float32)
        squares_part = jnp.sum(floats * floats, axis=1)
        logit_part = jnp.sum(floats * router_row, axis=1)
        scaled = (floats * gain_row).astype(jnp.bfloat16)
        gate_part = jnp.dot(scaled, gate_block, preferred_element_type=jnp.float32)
        up_part = jnp.dot(scaled, up_block, preferred_element_type=jnp.float32)
        squares, logits = lax.psum((squares_part, logit_part), "tp")
        gate_cut, up_cut = (
            lax.psum_scatter(gate_part, "tp", scatter_dimension=1, tiled=True),
            lax.psum_scatter(up_part, "tp", scatter_dimension=1, tiled=True),
        )
        inverse = lax.rsqrt(squares / D + EPSILON)[:, None]
        hidden = (jax.nn.silu(gate_cut * inverse) * (up_cut * inverse)).astype(jnp.bfloat16)
        partial_value = jnp.dot(
            lax.all_gather(hidden, "tp", axis=1, tiled=True),
            down_block,
            preferred_element_type=jnp.float32,
        )
        output = sum_groups(partial_value)
        router_gate = jax.nn.sigmoid(logits)[:, None]
        updated = (floats + router_gate * output).astype(jnp.bfloat16)
        is_live = jnp.arange(capacity, dtype=jnp.int32) < live_count
        new_rows = jnp.where(is_live[:, None], updated, picked)
        return stream.at[routed_ids].set(new_rows)

    def advance(step_index, carried):
        passed, finished = carried
        incoming = shifted(passed, "section", group_size)
        micro_index = step_index - layer_index
        active = (micro_index >= 0) & (micro_index < micro_count)
        clipped = jnp.clip(micro_index, 0, micro_count - 1)
        entering = lax.dynamic_index_in_dim(tokens_in, clipped, 0, keepdims=False)
        current = jnp.where(layer_index == 0, entering, incoming)
        result = apply_layer(current, clipped)
        store_now = active & (layer_index == LAYERS - 1)
        stored = lax.dynamic_update_index_in_dim(finished, result, clipped, 0)
        finished = jnp.where(store_now, stored, finished)
        return (result, finished)

    starting = (
        jnp.zeros((token_count, quarter), jnp.bfloat16),
        jnp.zeros((micro_count, token_count, quarter), jnp.bfloat16),
    )
    last_pass, finished = lax.fori_loop(0, total_steps, advance, starting)
    owned_span = token_count // group_size
    position_in_group = section_index - (LAYERS - 1) * group_size
    owner = jnp.arange(token_count, dtype=jnp.int32) // owned_span
    mine = (owner == position_in_group) & (layer_index == LAYERS - 1)
    contribution = jnp.where(mine[None, :, None], finished.astype(jnp.float32), 0.0)
    gathered = lax.psum_scatter(
        contribution.astype(jnp.bfloat16), "section", scatter_dimension=1, tiled=True
    )
    return gathered


def solution(mesh):
    return jax.shard_map(
        on_device,
        mesh=mesh,
        in_specs=(
            P(None, None, "tp"),
            P(None, "tp"),
            P(None, "tp"),
            P("section", "tp", None),
            P("section", "tp", None),
            P("section", None, "tp"),
            P(),
            P(),
        ),
        out_specs=P(None, "section", "tp"),
        check_vma=False,
    )
```

profile of v0, /device:TPU:0, one launch (start us, length us, event | category | flops | bytes accessed | tf_op | source)
XLA Modules:
  0.0 622.0 jit_solution(10781346180570471580)
XLA Ops:
  8.3 539.2 %while.19 = (s32[]{:T(128)}, bf16[224,1792]{1,0:T(8,128)(2,1)S(1)}, bf16[2,224,1792]{2,1,0:T(8,128)(2,1)S(1)}, pred[]{:T(512)}, s32[]{:T(128)}, /*index=5*/bf16[...) while((s32[]{:T(128)}, bf16[224,1792]{1,0:T(8,128)(2,1)S(1)}, ...), condition=%wide.region_8.9_spmd, body=%wide.region_0.8_spmd.sunk | while | flops 5556270592 | bytes 95513208 | solution.py:114
  13.5 17.0 %collective-permute-done = bf16[224,1792]{1,0:T(8,128)(2,1)S(1)} collective-permute-done((bf16[224,1792]{1,0:T(8,128)(2,1)S(1)}, bf16[224,1792]{1,0:T(8,128)(2,1)S(1)}, u32[]{:S(2)}, u32[]{:S(2)}) %collective-permute-start) | collective-permute-done | bytes 802848 | tf_op jit(solution)/shard_map/while/body/eval_jaxpr/ppermute | solution.py:22
  32.6 9.7 %fusion.43 = f32[112,4608]{1,0:T(8,128)} fusion(bf16[1792,4608]{1,0:T(8,128)(2,1)} %get-tuple-element.814, f32[1792]{0:T(1024)S(1)} %reduce.4, bf16[112,1792]{1,0:T(8,128)(2,1)S(1)} %gather_fusion, pred[112]{0:T(512)(128)(4,1)S(1)} %compare_and_fusion.3), kind=kOutput, calls=%fused_computation.25.clone.1 | convolution fusion | flops 1850490880 | bytes 18988144 | tf_op jit(solution)/shard_map/while/body/eval_jaxpr/dot_general | solution.py:76
  42.3 9.6 %fusion.44 = f32[112,4608]{1,0:T(8,128)} fusion(bf16[1792,4608]{1,0:T(8,128)(2,1)} %get-tuple-element.813, f32[1792]{0:T(1024)S(1)} %reduce.4, bf16[112,1792]{1,0:T(8,128)(2,1)S(1)} %gather_fusion, pred[112]{0:T(512)(128)(4,1)S(1)} %compare_and_fusion.3), kind=kOutput, calls=%fused_computation.26.clone.1 | convolution fusion | flops 1850490880 | bytes 18988144 | tf_op jit(solution)/shard_map/while/body/eval_jaxpr/dot_general | solution.py:75
  52.3 12.4 %all-reduce.3 = (f32[112]{0:T(128)S(1)}, f32[112]{0:T(128)S(1)}) all-reduce(f32[112]{0:T(128)S(1)} %get-tuple-element.752, f32[112]{0:T(128)S(1)} %get-tuple-element.753), channel_id=1, replica_groups=mesh['section'=8,'tp'=4] {'tp'}, use_global_device_ids=true, to_apply=%region_5.5 | all-reduce | flops 224 | bytes 1792 | tf_op jit(solution)/shard_map/while/body/eval_jaxpr/psum | solution.py:77
  64.7 23.2 %reduce-scatter.3.cloned.1.call-done = f32[112,1152]{1,0:T(8,128)} async-done(((f32[112,4608]{1,0:T(8,128)}), f32[112,1152]{1,0:T(8,128)}) %reduce-scatter.3.cloned.1.call-update) | async-done | bytes 516112 | tf_op jit(solution)/shard_map/while/body/eval_jaxpr/reduce_scatter | solution.py:80
  88.0 44.7 %reduce-scatter.5.cloned.1.call-done = f32[112,1152]{1,0:T(8,128)} async-done(((f32[112,4608]{1,0:T(8,128)}), f32[112,1152]{1,0:T(8,128)}) %reduce-scatter.5.cloned.1.call-update) | async-done | bytes 516112 | tf_op jit(solution)/shard_map/while/body/eval_jaxpr/reduce_scatter | solution.py:79
  134.0 20.8 %all_gather.12 = bf16[112,4608]{1,0:T(8,128)(2,1)S(1)} all-gather(bf16[112,1152]{1,0:T(8,128)(2,1)S(1)} %multiply_convert_fusion.2), channel_id=1, replica_groups=mesh['section'=8,'tp'=4] {'tp'}, dimensions={1}, use_global_device_ids=true | all-gather | bytes 1290240 | tf_op jit(solution)/shard_map/while/body/eval_jaxpr/all_gather | solution.py:85
  193.8 16.4 %collective-permute-done = bf16[224,1792]{1,0:T(8,128)(2,1)S(1)} collective-permute-done((bf16[224,1792]{1,0:T(8,128)(2,1)S(1)}, bf16[224,1792]{1,0:T(8,128)(2,1)S(1)}, u32[]{:S(2)}, u32[]{:S(2)}) %collective-permute-start) | collective-permute-done | bytes 802848 | tf_op jit(solution)/shard_map/while/body/eval_jaxpr/ppermute | solution.py:22
  212.4 9.6 %fusion.43 = f32[112,4608]{1,0:T(8,128)} fusion(bf16[1792,4608]{1,0:T(8,128)(2,1)} %get-tuple-element.814, f32[1792]{0:T(1024)S(1)} %reduce.4, bf16[112,1792]{1,0:T(8,128)(2,1)S(1)} %gather_fusion, pred[112]{0:T(512)(128)(4,1)S(1)} %compare_and_fusion.3), kind=kOutput, calls=%fused_computation.25.clone.1 | convolution fusion | flops 1850490880 | bytes 18988144 | tf_op jit(solution)/shard_map/while/body/eval_jaxpr/dot_general | solution.py:76
  222.1 9.6 %fusion.44 = f32[112,4608]{1,0:T(8,128)} fusion(bf16[1792,4608]{1,0:T(8,128)(2,1)} %get-tuple-element.813, f32[1792]{0:T(1024)S(1)} %reduce.4, bf16[112,1792]{1,0:T(8,128)(2,1)S(1)} %gather_fusion, pred[112]{0:T(512)(128)(4,1)S(1)} %compare_and_fusion.3), kind=kOutput, calls=%fused_computation.26.clone.1 | convolution fusion | flops 1850490880 | bytes 18988144 | tf_op jit(solution)/shard_map/while/body/eval_jaxpr/dot_general | solution.py:75
  232.0 11.5 %all-reduce.3 = (f32[112]{0:T(128)S(1)}, f32[112]{0:T(128)S(1)}) all-reduce(f32[112]{0:T(128)S(1)} %get-tuple-element.752, f32[112]{0:T(128)S(1)} %get-tuple-element.753), channel_id=1, replica_groups=mesh['section'=8,'tp'=4] {'tp'}, use_global_device_ids=true, to_apply=%region_5.5 | all-reduce | flops 224 | bytes 1792 | tf_op jit(solution)/shard_map/while/body/eval_jaxpr/psum | solution.py:77
  243.6 23.1 %reduce-scatter.3.cloned.1.call-done = f32[112,1152]{1,0:T(8,128)} async-done(((f32[112,4608]{1,0:T(8,128)}), f32[112,1152]{1,0:T(8,128)}) %reduce-scatter.3.cloned.1.call-update) | async-done | bytes 516112 | tf_op jit(solution)/shard_map/while/body/eval_jaxpr/reduce_scatter | solution.py:80
  266.6 44.5 %reduce-scatter.5.cloned.1.call-done = f32[112,1152]{1,0:T(8,128)} async-done(((f32[112,4608]{1,0:T(8,128)}), f32[112,1152]{1,0:T(8,128)}) %reduce-scatter.5.cloned.1.call-update) | async-done | bytes 516112 | tf_op jit(solution)/shard_map/while/body/eval_jaxpr/reduce_scatter | solution.py:79
  312.5 20.8 %all_gather.12 = bf16[112,4608]{1,0:T(8,128)(2,1)S(1)} all-gather(bf16[112,1152]{1,0:T(8,128)(2,1)S(1)} %multiply_convert_fusion.2), channel_id=1, replica_groups=mesh['section'=8,'tp'=4] {'tp'}, dimensions={1}, use_global_device_ids=true | all-gather | bytes 1290240 | tf_op jit(solution)/shard_map/while/body/eval_jaxpr/all_gather | solution.py:85
  372.4 16.4 %collective-permute-done = bf16[224,1792]{1,0:T(8,128)(2,1)S(1)} collective-permute-done((bf16[224,1792]{1,0:T(8,128)(2,1)S(1)}, bf16[224,1792]{1,0:T(8,128)(2,1)S(1)}, u32[]{:S(2)}, u32[]{:S(2)}) %collective-permute-start) | collective-permute-done | bytes 802848 | tf_op jit(solution)/shard_map/while/body/eval_jaxpr/ppermute | solution.py:22
  390.9 9.6 %fusion.43 = f32[112,4608]{1,0:T(8,128)} fusion(bf16[1792,4608]{1,0:T(8,128)(2,1)} %get-tuple-element.814, f32[1792]{0:T(1024)S(1)} %reduce.4, bf16[112,1792]{1,0:T(8,128)(2,1)S(1)} %gather_fusion, pred[112]{0:T(512)(128)(4,1)S(1)} %compare_and_fusion.3), kind=kOutput, calls=%fused_computation.25.clone.1 | convolution fusion | flops 1850490880 | bytes 18988144 | tf_op jit(solution)/shard_map/while/body/eval_jaxpr/dot_general | solution.py:76
  400.6 9.6 %fusion.44 = f32[112,4608]{1,0:T(8,128)} fusion(bf16[1792,4608]{1,0:T(8,128)(2,1)} %get-tuple-element.813, f32[1792]{0:T(1024)S(1)} %reduce.4, bf16[112,1792]{1,0:T(8,128)(2,1)S(1)} %gather_fusion, pred[112]{0:T(512)(128)(4,1)S(1)} %compare_and_fusion.3), kind=kOutput, calls=%fused_computation.26.clone.1 | convolution fusion | flops 1850490880 | bytes 18988144 | tf_op jit(solution)/shard_map/while/body/eval_jaxpr/dot_general | solution.py:75
  410.6 11.4 %all-reduce.3 = (f32[112]{0:T(128)S(1)}, f32[112]{0:T(128)S(1)}) all-reduce(f32[112]{0:T(128)S(1)} %get-tuple-element.752, f32[112]{0:T(128)S(1)} %get-tuple-element.753), channel_id=1, replica_groups=mesh['section'=8,'tp'=4] {'tp'}, use_global_device_ids=true, to_apply=%region_5.5 | all-reduce | flops 224 | bytes 1792 | tf_op jit(solution)/shard_map/while/body/eval_jaxpr/psum | solution.py:77
  421.9 23.3 %reduce-scatter.3.cloned.1.call-done = f32[112,1152]{1,0:T(8,128)} async-done(((f32[112,4608]{1,0:T(8,128)}), f32[112,1152]{1,0:T(8,128)}) %reduce-scatter.3.cloned.1.call-update) | async-done | bytes 516112 | tf_op jit(solution)/shard_map/while/body/eval_jaxpr/reduce_scatter | solution.py:80
  445.2 44.5 %reduce-scatter.5.cloned.1.call-done = f32[112,1152]{1,0:T(8,128)} async-done(((f32[112,4608]{1,0:T(8,128)}), f32[112,1152]{1,0:T(8,128)}) %reduce-scatter.5.cloned.1.call-update) | async-done | bytes 516112 | tf_op jit(solution)/shard_map/while/body/eval_jaxpr/reduce_scatter | solution.py:79
  491.2 20.8 %all_gather.12 = bf16[112,4608]{1,0:T(8,128)(2,1)S(1)} all-gather(bf16[112,1152]{1,0:T(8,128)(2,1)S(1)} %multiply_convert_fusion.2), channel_id=1, replica_groups=mesh['section'=8,'tp'=4] {'tp'}, dimensions={1}, use_global_device_ids=true | all-gather | bytes 1290240 | tf_op jit(solution)/shard_map/while/body/eval_jaxpr/all_gather | solution.py:85
  536.0 8.8 %collective-permute-done.4 = f32[112,896]{1,0:T(8,128)} collective-permute-done((f32[112,896]{1,0:T(8,128)S(1)}, f32[112,896]{1,0:T(8,128)}, u32[]{:S(2)}, u32[]{:S(2)}) %collective-permute-start.4) | collective-permute-done | bytes 401440 | tf_op jit(solution)/shard_map/while/body/eval_jaxpr/ppermute | solution.py:16
  555.3 57.5 %all-reduce.6.cloned.1.call-done = bf16[2,224,1792]{2,0,1:T(2,128)(2,1)} async-done(((bf16[2,224,1792]{2,0,1:T(2,128)(2,1)}), bf16[2,224,1792]{2,0,1:T(2,128)(2,1)}) %all-reduce.6.cloned.1.call-update) | async-done | bytes 1605648
  (116 shorter events, 131.1 us)
Async XLA Ops:
  7.4 1.0 copy-start.1
  8.4 79.6 %reduce-scatter.3.cloned.1.call-start = ((), (), s32[]{:S(2)}) async-start(), calls=%async_computation.3 | async-start | bytes 2580480 | tf_op jit(solution)/shard_map/while/body/eval_jaxpr/reduce_scatter | solution.py:80
  8.4 22.0 %collective-permute-start = (bf16[224,1792]{1,0:T(8,128)(2,1)S(1)}, bf16[224,1792]{1,0:T(8,128)(2,1)S(1)}, u32[]{:S(2)}, u32[]{:S(2)}) collective-permute-start(bf16[224,1792]{1,0:T(8,128)(2,1)S(1)} %get-tuple-element.779), channel_id=1, source_target_pairs={{0,16},{4,20},{8,24},{12,28},{1,17},{5,21},{9,25},{13,29},{2,18},{... | collective-permute-start | bytes 2408456 | tf_op jit(solution)/shard_map/while/body/eval_jaxpr/ppermute | solution.py:22
  42.2 90.4 %reduce-scatter.5.cloned.1.call-start = ((), (), s32[]{:S(2)}) async-start(), calls=%async_computation.4 | async-start | bytes 2580480 | tf_op jit(solution)/shard_map/while/body/eval_jaxpr/reduce_scatter | solution.py:79
  162.9 9.6 %collective-permute-start.1 = (f32[112,896]{1,0:T(8,128)S(1)}, f32[112,896]{1,0:T(8,128)S(1)}, u32[]{:S(2)}, u32[]{:S(2)}) collective-permute-start(f32[112,896]{1,0:T(8,128)S(1)} %slice_select_fusion.4), channel_id=1, source_target_pairs={{0,8},{4,12},{8,0},{12,4},{16,24},{20,28},{24,16},{28,20},{1,9},{5... | collective-permute-start | bytes 1204232 | tf_op jit(solution)/shard_map/while/body/eval_jaxpr/ppermute | solution.py:16
  172.7 1.6 collective-permute-start.2
  174.4 1.6 collective-permute-start.3
  176.2 11.5 %collective-permute-start.4 = (f32[112,896]{1,0:T(8,128)S(1)}, f32[112,896]{1,0:T(8,128)}, u32[]{:S(2)}, u32[]{:S(2)}) collective-permute-start(f32[112,896]{1,0:T(8,128)S(1)} %maximum_select_fusion.3), channel_id=1, source_target_pairs={{0,8},{4,12},{8,0},{12,4},{16,24},{20,28},{24,16},{28,20},{1,9},{5... | collective-permute-start | bytes 1204232 | tf_op jit(solution)/shard_map/while/body/eval_jaxpr/ppermute | solution.py:16
  190.4 76.2 %reduce-scatter.3.cloned.1.call-start = ((), (), s32[]{:S(2)}) async-start(), calls=%async_computation.3 | async-start | bytes 2580480 | tf_op jit(solution)/shard_map/while/body/eval_jaxpr/reduce_scatter | solution.py:80
  190.4 19.8 %collective-permute-start = (bf16[224,1792]{1,0:T(8,128)(2,1)S(1)}, bf16[224,1792]{1,0:T(8,128)(2,1)S(1)}, u32[]{:S(2)}, u32[]{:S(2)}) collective-permute-start(bf16[224,1792]{1,0:T(8,128)(2,1)S(1)} %get-tuple-element.779), channel_id=1, source_target_pairs={{0,16},{4,20},{8,24},{12,28},{1,17},{5,21},{9,25},{13,29},{2,18},{... | collective-permute-start | bytes 2408456 | tf_op jit(solution)/shard_map/while/body/eval_jaxpr/ppermute | solution.py:22
  222.0 89.1 %reduce-scatter.5.cloned.1.call-start = ((), (), s32[]{:S(2)}) async-start(), calls=%async_computation.4 | async-start | bytes 2580480 | tf_op jit(solution)/shard_map/while/body/eval_jaxpr/reduce_scatter | solution.py:79
  341.4 9.5 %collective-permute-start.1 = (f32[112,896]{1,0:T(8,128)S(1)}, f32[112,896]{1,0:T(8,128)S(1)}, u32[]{:S(2)}, u32[]{:S(2)}) collective-permute-start(f32[112,896]{1,0:T(8,128)S(1)} %slice_select_fusion.4), channel_id=1, source_target_pairs={{0,8},{4,12},{8,0},{12,4},{16,24},{20,28},{24,16},{28,20},{1,9},{5... | collective-permute-start | bytes 1204232 | tf_op jit(solution)/shard_map/while/body/eval_jaxpr/ppermute | solution.py:16
  351.1 1.6 collective-permute-start.2
  352.8 1.6 collective-permute-start.3
  354.6 11.5 %collective-permute-start.4 = (f32[112,896]{1,0:T(8,128)S(1)}, f32[112,896]{1,0:T(8,128)}, u32[]{:S(2)}, u32[]{:S(2)}) collective-permute-start(f32[112,896]{1,0:T(8,128)S(1)} %maximum_select_fusion.3), channel_id=1, source_target_pairs={{0,8},{4,12},{8,0},{12,4},{16,24},{20,28},{24,16},{28,20},{1,9},{5... | collective-permute-start | bytes 1204232 | tf_op jit(solution)/shard_map/while/body/eval_jaxpr/ppermute | solution.py:16
  368.8 76.5 %reduce-scatter.3.cloned.1.call-start = ((), (), s32[]{:S(2)}) async-start(), calls=%async_computation.3 | async-start | bytes 2580480 | tf_op jit(solution)/shard_map/while/body/eval_jaxpr/reduce_scatter | solution.py:80
  368.8 20.0 %collective-permute-start = (bf16[224,1792]{1,0:T(8,128)(2,1)S(1)}, bf16[224,1792]{1,0:T(8,128)(2,1)S(1)}, u32[]{:S(2)}, u32[]{:S(2)}) collective-permute-start(bf16[224,1792]{1,0:T(8,128)(2,1)S(1)} %get-tuple-element.779), channel_id=1, source_target_pairs={{0,16},{4,20},{8,24},{12,28},{1,17},{5,21},{9,25},{13,29},{2,18},{... | collective-permute-start | bytes 2408456 | tf_op jit(solution)/shard_map/while/body/eval_jaxpr/ppermute | solution.py:22
  400.6 89.2 %reduce-scatter.5.cloned.1.call-start = ((), (), s32[]{:S(2)}) async-start(), calls=%async_computation.4 | async-start | bytes 2580480 | tf_op jit(solution)/shard_map/while/body/eval_jaxpr/reduce_scatter | solution.py:79
  520.1 9.6 %collective-permute-start.1 = (f32[112,896]{1,0:T(8,128)S(1)}, f32[112,896]{1,0:T(8,128)S(1)}, u32[]{:S(2)}, u32[]{:S(2)}) collective-permute-start(f32[112,896]{1,0:T(8,128)S(1)} %slice_select_fusion.4), channel_id=1, source_target_pairs={{0,8},{4,12},{8,0},{12,4},{16,24},{20,28},{24,16},{28,20},{1,9},{5... | collective-permute-start | bytes 1204232 | tf_op jit(solution)/shard_map/while/body/eval_jaxpr/ppermute | solution.py:16
  529.9 1.6 collective-permute-start.2
  531.5 1.6 collective-permute-start.3
  533.3 11.5 %collective-permute-start.4 = (f32[112,896]{1,0:T(8,128)S(1)}, f32[112,896]{1,0:T(8,128)}, u32[]{:S(2)}, u32[]{:S(2)}) collective-permute-start(f32[112,896]{1,0:T(8,128)S(1)} %maximum_select_fusion.3), channel_id=1, source_target_pairs={{0,8},{4,12},{8,0},{12,4},{16,24},{20,28},{24,16},{28,20},{1,9},{5... | collective-permute-start | bytes 1204232 | tf_op jit(solution)/shard_map/while/body/eval_jaxpr/ppermute | solution.py:16
  547.5 65.3 %all-reduce.6.cloned.1.call-start = ((), (), s32[]{:S(2)}) async-start(), calls=%async_computation.2 | async-start | bytes 3211264
  547.6 6.5 %copy-start.2 = (u32[32]{0:T(128)S(1)}, u32[32]{0:T(128)}, u32[]{:S(2)}) copy-start(u32[32]{0:T(128)} %constant.243) | copy-start | bytes 388
  (1 other events, 1.0 us)
Sparse Core Ops, SparseCore 0:
  42.4 45.5 reduce-scatter.2
  90.3 42.2 reduce-scatter.4
  222.1 44.4 reduce-scatter.2
  268.8 42.2 reduce-scatter.4
  400.7 44.5 reduce-scatter.2
  447.4 42.3 reduce-scatter.4
Sparse Core Ops, SparseCore 1:
  554.1 58.6 all-reduce.5
where the time goes:
time: 623 us; the launch traced here: 622 us
  waiting for transfers between devices  370 us (59%)
  blocking collectives  97.6 us (16%)
  matrix products  81.9 us (13%)
  other arithmetic  27.2 us (4%)
  starting transfers between devices  21.9 us (4%)
  between operations  15.5 us (2%)
  local copies, waits for them, and re-layouts  7.69 us (1%)
    reduce_scatter x3, waiting for transfers between devices, apply_layer(): lax.psum_scatter(gate_part, 'tp', scatter_dimension=1, tiled=True)  134 us
    reduce_scatter x3, waiting for transfers between devices, apply_layer(): lax.psum_scatter(up_part, 'tp', scatter_dimension=1, tiled=True)  69.6 us
    all_gather x3, blocking collectives, apply_layer(): lax.all_gather(hidden, 'tp', axis=1, tiled=True)  62.3 us
    ppermute x12, waiting for transfers between devices, swapped(): return lax.ppermute(value, axis, pairs)  58.8 us
    unnamed x2, waiting for transfers between devices  57.5 us
    ppermute x3, waiting for transfers between devices, shifted(): return lax.ppermute(value, axis, pairs)  49.9 us
    psum x3, blocking collectives, apply_layer(): squares, logits = lax.psum((squares_part, logit_part), 'tp')  35.3 us
    dot_general x3, matrix products, apply_layer(): up_part = jnp.dot(scaled, up_block, preferred_element_type=jnp.float32)  28.9 us
  transfers between devices with their start and end apart: 22, of which 22 were waited for; matrix products, arithmetic and copies ran while one was open for 6% of the time, Pallas kernels for 0%

commit v1 on v0

v1 whole, which is shorter than its diff:
```python
import jax
import jax.numpy as jnp
from jax import lax
from jax.experimental import pallas as pl
from jax.experimental.pallas import tpu as pltpu
from jax.sharding import PartitionSpec as P


LAYERS = 2
EPSILON = 1e-06
LANES = 128
F32 = jnp.float32
BF16 = jnp.bfloat16


def swapped(value, axis, mask):
    pairs = [(i, i ^ mask) for i in range(lax.axis_size(axis))]
    return lax.ppermute(value, axis, pairs)


def layer_swapped(value, layer, section_mask, tp_mask):
    tp_size = lax.axis_size("tp")
    group_size = lax.axis_size("section") // LAYERS
    pairs = []
    for s in range(layer * group_size, (layer + 1) * group_size):
        for t in range(tp_size):
            pairs.append((s * tp_size + t, (s ^ section_mask) * tp_size + (t ^ tp_mask)))
    return lax.ppermute(value, ("section", "tp"), pairs)


def sent_to_others(value, layer):
    tp_size = lax.axis_size("tp")
    group_size = lax.axis_size("section") // LAYERS
    pairs = []
    for s in range(layer * group_size, (layer + 1) * group_size):
        for t in range(tp_size):
            pairs.append((s * tp_size + t, (s ^ group_size) * tp_size + t))
    return lax.ppermute(value, ("section", "tp"), pairs)


def row_cuts(rows):
    helped = rows * 2 // 7 // 16 * 16
    first = ((rows - helped) // 2 + 15) // 16 * 16
    return [(0, first), (first, rows - helped), (rows - helped, rows)]


def in_hbm(value):
    return pltpu.with_memory_space_constraint(value, pltpu.HBM)


def block_of(extent, most, step):
    best = step
    for size in range(step, min(extent, most) + 1, step):
        if extent % size == 0:
            best = size
    return best


def front_half(scaled, gate_block, up_block, half, active, cuts):
    rows, depth = scaled.shape
    width = gate_block.shape[1] // 2
    if width % LANES:
        picked = [lax.dynamic_slice_in_dim(w, half * width, width, 1) for w in (gate_block, up_block)]
        both = jnp.stack([jnp.dot(scaled, w, preferred_element_type=F32).astype(BF16) for w in picked])
        return [both[:, lo:hi] for lo, hi in cuts]
    cols = block_of(width, 768, LANES)
    steps = width // cols

    def kernel(half_ref, x_ref, g_ref, u_ref, *o_refs):
        @pl.when(half_ref[1] == 1)
        def _():
            x = x_ref[...]
            for i, w_ref in enumerate((g_ref, u_ref)):
                product = jnp.dot(x, w_ref[...], preferred_element_type=F32).astype(BF16)
                for (lo, hi), o_ref in zip(cuts, o_refs):
                    o_ref[i] = product[lo:hi]

    weight_spec = pl.BlockSpec((depth, cols), lambda i, h: (0, (h[0] * steps + i) * h[1]))
    return pl.pallas_call(
        kernel,
        out_shape=[jax.ShapeDtypeStruct((2, hi - lo, width), BF16) for lo, hi in cuts],
        grid_spec=pltpu.PrefetchScalarGridSpec(
            num_scalar_prefetch=1,
            grid=(steps,),
            in_specs=[pl.BlockSpec((rows, depth), lambda i, h: (0, 0)), weight_spec, weight_spec],
            out_specs=[pl.BlockSpec((2, hi - lo, cols), lambda i, h: (0, 0, i)) for lo, hi in cuts],
        ),
        cost_estimate=pl.CostEstimate(
            flops=4 * rows * depth * width, bytes_accessed=4 * depth * width, transcendentals=0
        ),
        compiler_params=pltpu.CompilerParams(vmem_limit_bytes=32 * 2**20),
        name="front_half",
    )(jnp.stack([half, active]), scaled, in_hbm(gate_block), in_hbm(up_block))


def back_half(hidden, down_block, half, side, active, base=None):
    rows, depth = hidden.shape
    cols = down_block.shape[1] // 2
    if depth % LANES or cols % LANES:
        results = []
        for i in range(2):
            column = (1 - side if i == 0 else side) * cols
            picked = lax.dynamic_slice(down_block, (half * depth, column), (depth, cols))
            result = jnp.dot(hidden, picked, preferred_element_type=F32)
            results.append(result if base is None else result + base[i].astype(F32))
        return results[0] if base is None else results[0].astype(BF16), results[1]
    held_as = (F32, F32) if base is None else (BF16, F32)

    def kernel(half_ref, x_ref, w_ref, *refs):
        for i, o_ref in enumerate(refs[-2:]):

            @pl.when((pl.program_id(0) == i) & (half_ref[2] == 1))
            def _():
                product = jnp.dot(x_ref[...], w_ref[...], preferred_element_type=F32)
                if base is not None:
                    product = product + refs[i][...]
                o_ref[...] = product.astype(held_as[i])

    whole = pl.BlockSpec((rows, cols), lambda i, h: (0, 0))
    in_specs = [
        pl.BlockSpec((rows, depth), lambda i, h: (0, 0)),
        pl.BlockSpec((depth, cols), lambda i, h: (h[0] * h[2], jnp.where(i == h[2], h[1], 1 - h[1]))),
    ]
    operands = [hidden, in_hbm(down_block)]
    if base is not None:
        in_specs += [whole, whole]
        operands += list(base)
    return pl.pallas_call(
        kernel,
        out_shape=[jax.ShapeDtypeStruct((rows, cols), t) for t in held_as],
        grid_spec=pltpu.PrefetchScalarGridSpec(
            num_scalar_prefetch=1, grid=(2,), in_specs=in_specs, out_specs=[whole, whole]
        ),
        cost_estimate=pl.CostEstimate(
            flops=4 * rows * depth * cols, bytes_accessed=4 * depth * cols, transcendentals=0
        ),
        compiler_params=pltpu.CompilerParams(vmem_limit_bytes=32 * 2**20),
        name="back_half",
    )(jnp.stack([half, side, active]), *operands)


def joined(own, other, upper):
    return jnp.where(
        upper, jnp.concatenate([other, own], axis=-1), jnp.concatenate([own, other], axis=-1)
    )


def on_device(
    tokens_in,
    norm_gain,
    router_weight,
    gate_weight,
    up_weight,
    down_weight,
    routed_rows,
    routed_count,
):
    micro_count, token_count, quarter = tokens_in.shape
    capacity = routed_rows.shape[2]
    model_width = quarter * lax.axis_size("tp")
    section_index = lax.axis_index("section")
    section_size = lax.axis_size("section")
    group_size = section_size // LAYERS
    layer_index = section_index // group_size
    tp_index = lax.axis_index("tp")
    tp_bits = lax.axis_size("tp").bit_length() - 1
    gate_block = gate_weight[0]
    up_block = up_weight[0]
    down_block = down_weight[0]
    pair_bit = (tp_index % 2).astype(jnp.int32)
    core_bit = section_index % 2

    def summed_over_tp(value):
        for bit in range(tp_bits):
            other = swapped(value, "tp", 2**bit)
            value = value + other
        return value

    def row_sums(picked, k):
        floats = picked.astype(F32)
        return jnp.stack([jnp.sum(floats * floats, axis=1), jnp.sum(floats * router_weight[k], axis=1)])

    def cross_sums(parts, plane):
        for bit in range(1, tp_bits):
            width = parts[0].shape[2] // 2
            side = tp_index // 2**bit % 2
            give = sum(
                lax.dynamic_slice_in_dim(p, (1 - side) * width, width, 2).astype(F32) for p in parts
            ).astype(BF16)
            parts = [lax.dynamic_slice_in_dim(p, side * width, width, 2) for p in parts]
            parts.append(layer_swapped(give, plane, 0, 2**bit))
        return parts

    def hidden_halves(parts, inverse, plane):
        total = sum(p.astype(F32) for p in parts)
        gate = total[0] * inverse
        hidden = (jax.nn.silu(gate) * (total[1] * inverse)).astype(BF16)
        for bit in reversed(range(1, tp_bits)):
            upper = tp_index // 2**bit % 2 == 1
            other = layer_swapped(hidden, plane, 0, 2**bit)
            hidden = joined(hidden, other, upper)
        return hidden, layer_swapped(hidden, plane, 0, 1)

    def layer_output(picked, squares, k):
        on_layer = layer_index == k
        active = on_layer.astype(jnp.int32)
        helper = LAYERS - 1 - k
        cuts = row_cuts(picked.shape[0])
        planes = (k, k, helper)
        scaled = (picked.astype(F32) * norm_gain[k]).astype(BF16)
        inverse = lax.rsqrt(squares / model_width + EPSILON)[:, None]
        given = list(front_half(scaled, gate_block, up_block, 1 - pair_bit, active, cuts))
        given[2] = sent_to_others(given[2], k)
        kept = list(front_half(scaled, gate_block, up_block, pair_bit, active, cuts))
        kept[2] = sent_to_others(kept[2], k)
        halves = []
        for i, (lo, hi) in enumerate(cuts):
            received = layer_swapped(given[i], planes[i], 0, 1)
            parts = cross_sums([kept[i], received], planes[i])
            halves.append(hidden_halves(parts, inverse[lo:hi], planes[i]))
        own_h = sent_to_others(halves[2][0], helper)
        other_h = sent_to_others(halves[2][1], helper)
        own = jnp.concatenate([halves[0][0], halves[1][0], own_h])
        other = jnp.concatenate([halves[0][1], halves[1][1], other_h])
        base = back_half(own, down_block, pair_bit, core_bit, active)
        give, keep = back_half(other, down_block, 1 - pair_bit, core_bit, active, base)
        got = layer_swapped(give, k, 1, 0)
        piece = (keep + got.astype(F32)).astype(BF16)
        middle = piece.shape[0] // 2
        bits = [2**b for b in range(1, group_size.bit_length() - 1)]
        one = sent_to_others(piece[:middle], k)
        one = jnp.where(on_layer, piece[:middle], one)
        two = piece[middle:]
        for bit in bits:
            got = layer_swapped(two, k, bit, 0)
            two = (two.astype(F32) + got.astype(F32)).astype(BF16)
        for bit in bits:
            got = swapped(one, "section", bit)
            one = (one.astype(F32) + got.astype(F32)).astype(BF16)
        got = sent_to_others(two, k)
        two = jnp.where(on_layer, two, got)
        upper = core_bit == 1
        return jnp.concatenate(
            [joined(v, swapped(v, "section", 1), upper) for v in (one, two)]
        )

    def places(ids, wanted):
        same = wanted[:, None] == ids[None, :]
        at = jnp.sum(jnp.where(same, jnp.arange(ids.shape[0], dtype=jnp.int32)[None, :], 0), axis=1)
        return jnp.any(same, axis=1)[:, None], at

    def taken(source, at):
        return jnp.take(source, at, axis=0, mode="clip")

    rows_all = micro_count * capacity
    stream = tokens_in.reshape(micro_count * token_count, quarter)
    first_token = jnp.arange(micro_count, dtype=jnp.int32)[:, None] * token_count
    span = token_count // section_size
    held = (first_token + section_index * span + jnp.arange(span, dtype=jnp.int32)).reshape(-1)
    result = lax.dynamic_slice_in_dim(tokens_in, section_index * span, span, 1)
    result = result.reshape(micro_count * span, quarter)
    done = []
    for k in range(LAYERS):
        ids = (routed_rows[:, k] + first_token).reshape(rows_all)
        live = jnp.arange(capacity, dtype=jnp.int32)[None] < routed_count[:, k][:, None]
        picked = taken(stream, ids)
        for earlier_ids, earlier_rows in done:
            found, at = places(earlier_ids, ids)
            picked = jnp.where(found, taken(earlier_rows, at), picked)
        sums = summed_over_tp(row_sums(picked, k))
        output = layer_output(picked, sums[0], k)
        router_gate = jax.nn.sigmoid(sums[1])[:, None]
        updated = (picked.astype(F32) + router_gate * output.astype(F32)).astype(BF16)
        rows = jnp.where(live.reshape(rows_all, 1), updated, picked)
        done.append((ids, rows))
        found, at = places(ids, held)
        result = jnp.where(found, taken(rows, at), result)
    return result.reshape(micro_count, span, quarter)


def solution(mesh):
    return jax.shard_map(
        on_device,
        mesh=mesh,
        in_specs=(
            P(None, None, "tp"),
            P(None, "tp"),
            P(None, "tp"),
            P("section", "tp", None),
            P("section", "tp", None),
            P("section", None, "tp"),
            P(),
            P(),
        ),
        out_specs=P(None, "section", "tp"),
        check_vma=False,
    )
```

time: 623 us -> 323 us (0.52)
  waiting for transfers between devices: 370 us -> 132 us
  blocking collectives: 97.6 us -> 0 us
  matrix products: 81.9 us -> 0 us
  starting transfers between devices: 21.9 us -> 101 us
  Pallas kernels: 0 us -> 43.8 us
  local copies, waits for them, and re-layouts: 7.69 us -> 23.6 us
  between operations: 15.5 us -> 1.03 us
  other arithmetic: 27.2 us -> 20.6 us
    reduce_scatter x6 -> x0, waiting for transfers between devices: 203 us -> none  [the longest x3 134 us: apply_layer(): lax.psum_scatter(gate_part, 'tp', scatter_dimension=1, tiled=True)]
    dot_general x9 -> x0, matrix products: 81.9 us -> none  [the longest x3 28.9 us: apply_layer(): up_part = jnp.dot(scaled, up_block, preferred_element_type=jnp.float32)]
    ppermute x3 -> x40, starting transfers between devices: 11.7 us -> 89.6 us  [the longest x28 49.9 us: layer_swapped(): return lax.ppermute(value, ('section', 'tp'), pairs)]
    ppermute x3 -> x40, waiting for transfers between devices: 49.9 us -> 114 us  [the longest x28 58.4 us: layer_swapped(): return lax.ppermute(value, ('section', 'tp'), pairs)]
    all_gather x3 -> x0, blocking collectives: 62.3 us -> none  [apply_layer(): lax.all_gather(hidden, 'tp', axis=1, tiled=True)]
    unnamed x2 -> x0, waiting for transfers between devices: 57.5 us -> none
    pallas_call x0 -> x8, Pallas kernels: none -> 43.8 us  [the longest x4 25.3 us: front_half(): pl.pallas_call(kernel, out_shape=[jax.ShapeDtypeStruct((2, hi - lo, width...]
    ppermute x12 -> x10, waiting for transfers between devices: 58.8 us -> 18.3 us  [swapped(): return lax.ppermute(value, axis, pairs)]
  transfers between devices with their start and end apart: 22 -> 50, of which waited for: 22 -> 21; matrix products, arithmetic and copies ran while one was open for 6% -> 9% of each run, Pallas kernels for 0% -> 8%
where the time goes in v1:
time: 323 us; the launch traced here: 322 us
  waiting for transfers between devices  132 us (41%)
  starting transfers between devices  101 us (31%)
  Pallas kernels  43.8 us (14%)
  local copies, waits for them, and re-layouts  23.6 us (7%)
  other arithmetic  20.6 us (6%)
    ppermute x28, waiting for transfers between devices, layer_swapped(): return lax.ppermute(value, ('section', 'tp'), pairs)  58.4 us
    ppermute x12, waiting for transfers between devices, sent_to_others(): return lax.ppermute(value, ('section', 'tp'), pairs)  55.3 us
    ppermute x28, starting transfers between devices, layer_swapped(): return lax.ppermute(value, ('section', 'tp'), pairs)  49.9 us
    ppermute x12, starting transfers between devices, sent_to_others(): return lax.ppermute(value, ('section', 'tp'), pairs)  39.6 us
    pallas_call x4, Pallas kernels, front_half(): pl.pallas_call(kernel, out_shape=[jax.ShapeDtypeStruct((2, hi - lo, width...  25.3 us
    pallas_call x4, Pallas kernels, back_half(): pl.pallas_call(kernel, out_shape=[jax.ShapeDtypeStruct((rows, cols), t) f...  18.5 us
    ppermute x10, waiting for transfers between devices, swapped(): return lax.ppermute(value, axis, pairs)  18.3 us
    ppermute x10, starting transfers between devices, swapped(): return lax.ppermute(value, axis, pairs)  11.4 us
  transfers between devices with their start and end apart: 50, of which 21 were waited for; matrix products, arithmetic and copies ran while one was open for 9% of the time, Pallas kernels for 8%

profile of v1, /device:TPU:0, one launch (start us, length us, event | category | flops | bytes accessed | tf_op | source)
XLA Modules:
  0.0 322.0 jit_solution(16160065639654548676)
XLA Ops:
  8.4 9.6 %front_half.5 = (bf16[2,80,2304]{2,1,0:T(8,128)(2,1)S(1)}, bf16[2,80,2304]{2,1,0:T(8,128)(2,1)S(1)}, bf16[2,64,2304]{2,1,0:T(8,128)(2,1)}) custom-call(s32[2]{0:T(128)S(1)} %get-tuple-element.81.half_ref, bf16[224,1792]{1,0:T(8,128)(2,1)S(1)} %get-tuple-element.62.x_ref, bf16[1792,4608]{1,0:T(8,128)(2,1)} %bitcast.119, bf16[1792,4608]{1,0:T(8,128)(2,1)} %bitcast.123), custom_call_target="tpu_custom_call" | custom-call | flops 3699376128 | bytes 16515072 | tf_op jit(solution)/shard_map/front_half/pallas_call | solution.py:79
  20.1 8.8 %front_half.4 = (bf16[2,80,2304]{2,1,0:T(8,128)(2,1)S(1)}, bf16[2,80,2304]{2,1,0:T(8,128)(2,1)S(1)}, bf16[2,64,2304]{2,1,0:T(8,128)(2,1)S(1)}) custom-call(s32[2]{0:T(128)S(1)} %get-tuple-element.82.half_ref, bf16[224,1792]{1,0:T(8,128)(2,1)S(1)} %get-tuple-element.62.x_ref, bf16[1792,4608]{1,0:T(8,128)(2,1)} %bitcast.120, bf16[1792,4608]{1,0:T(8,128)(2,1)} %bitcast.124), custom_call_target="tpu_custom_call" | custom-call | flops 3699376128 | bytes 16515072 | tf_op jit(solution)/shard_map/front_half/pallas_call | solution.py:79
  53.1 4.6 %gather_fusion.2 = bf16[224,1792]{1,0:T(8,128)(2,1)} fusion(bf16[448,1792]{1,0:T(8,128)(2,1)} %bitcast.128, s32[1024]{0:T(1024)} %pad_clamp_fusion.2), kind=kCustom, calls=%fused_computation.2 | custom fusion | bytes 1606528 | tf_op jit(solution)/shard_map/jit(_take)/gather | solution.py:253
  57.7 10.4 %collective-permute-done.1 = f32[2,224]{1,0:T(2,128)} collective-permute-done((f32[2,224]{1,0:T(2,128)}, f32[2,224]{1,0:T(2,128)}, u32[]{:S(2)}, u32[]{:S(2)}) %collective-permute-start.1) | collective-permute-done | bytes 1824 | tf_op jit(solution)/shard_map/ppermute | solution.py:18
  70.0 5.4 %collective-permute-start.7 = (bf16[2,80,1152]{2,1,0:T(8,128)(2,1)S(1)}, bf16[2,80,1152]{2,1,0:T(8,128)(2,1)S(1)}, u32[]{:S(2)}, u32[]{:S(2)}) collective-permute-start(bf16[2,80,1152]{2,1,0:T(8,128)(2,1)S(1)} %add_convert_fusion.4), channel_id=1, source_target_pairs={{0,2},{1,3},{2,0},{3,1},{4,6},{5,7},{6,4},{7,5},{8,10},{9,11},{10,... | collective-permute-start | bytes 1105928 | tf_op jit(solution)/shard_map/ppermute | solution.py:28
  79.2 21.4 %collective-permute-done.7 = bf16[2,80,1152]{2,1,0:T(8,128)(2,1)S(1)} collective-permute-done((bf16[2,80,1152]{2,1,0:T(8,128)(2,1)S(1)}, bf16[2,80,1152]{2,1,0:T(8,128)(2,1)S(1)}, u32[]{:S(2)}, u32[]{:S(2)}) %collective-permute-start.7) | collective-permute-done | bytes 368672 | tf_op jit(solution)/shard_map/ppermute | solution.py:28
  103.9 8.6 %collective-permute-done.3 = bf16[2,80,1152]{2,1,0:T(8,128)(2,1)S(1)} collective-permute-done((bf16[2,80,1152]{2,1,0:T(8,128)(2,1)S(1)}, bf16[2,80,1152]{2,1,0:T(8,128)(2,1)S(1)}, u32[]{:S(2)}, u32[]{:S(2)}) %collective-permute-start.3) | collective-permute-done | bytes 368672 | tf_op jit(solution)/shard_map/ppermute | solution.py:28
  119.5 4.1 %collective-permute-start.9 = (bf16[80,2304]{1,0:T(8,128)(2,1)S(1)}, bf16[80,2304]{1,0:T(8,128)(2,1)S(1)}, u32[]{:S(2)}, u32[]{:S(2)}) collective-permute-start(bf16[80,2304]{1,0:T(8,128)(2,1)S(1)} %maximum_select_fusion.5), channel_id=1, source_target_pairs={{0,1},{1,0},{2,3},{3,2},{4,5},{5,4},{6,7},{7,6},{8,9},{9,8},{10,11... | collective-permute-start | bytes 1105928 | tf_op jit(solution)/shard_map/ppermute | solution.py:28
  129.3 6.9 %collective-permute-done.17 = bf16[64,2304]{1,0:T(8,128)(2,1)S(1)} collective-permute-done((bf16[64,2304]{1,0:T(8,128)(2,1)S(1)}, bf16[64,2304]{1,0:T(8,128)(2,1)S(1)}, u32[]{:S(2)}, u32[]{:S(2)}) %collective-permute-start.17) | collective-permute-done | bytes 294944 | tf_op jit(solution)/shard_map/ppermute | solution.py:38
  136.3 5.3 %back_half.4 = (f32[224,896]{1,0:T(8,128)S(1)}, f32[224,896]{1,0:T(8,128)S(1)}) custom-call(s32[3]{0:T(128)S(1)} %pad_add_fusion.2.half_ref, bf16[224,2304]{1,0:T(8,128)(2,1)S(1)} %pad_maximum_fusion.1.x_ref, bf16[4608,1792]{1,0:T(8,128)(2,1)} %bitcast.115), custom_call_target="tpu_custom_call" | custom-call | flops 1849688064 | bytes 8257536 | tf_op jit(solution)/shard_map/back_half/pallas_call | solution.py:128
  141.7 5.3 %back_half.5 = (bf16[224,896]{1,0:T(8,128)(2,1)S(1)}, f32[224,896]{1,0:T(8,128)S(1)}) custom-call(s32[3]{0:T(128)S(1)} %pad_add_fusion.3.half_ref, bf16[224,2304]{1,0:T(8,128)(2,1)S(1)} %pad_maximum_fusion.x_ref, bf16[4608,1792]{1,0:T(8,128)(2,1)} %bitcast.116, f32[224,896]{1,0:T(8,128)S(1)} %get-tuple-element.31.refs_0_, ...), custom_call_target="tpu_custom_call" | custom-call | flops 1849688064 | bytes 8257536 | tf_op jit(solution)/shard_map/back_half/pallas_call | solution.py:128
  152.1 4.7 %collective-permute-done.19 = bf16[112,896]{1,0:T(8,128)(2,1)S(1)} collective-permute-done((bf16[112,896]{1,0:T(8,128)(2,1)S(1)}, bf16[112,896]{1,0:T(8,128)(2,1)S(1)}, u32[]{:S(2)}, u32[]{:S(2)}) %collective-permute-start.19) | collective-permute-done | bytes 200736 | tf_op jit(solution)/shard_map/ppermute | solution.py:38
  161.1 5.5 %collective-permute-done.22 = bf16[112,896]{1,0:T(8,128)(2,1)S(1)} collective-permute-done((bf16[112,896]{1,0:T(8,128)(2,1)S(1)}, bf16[112,896]{1,0:T(8,128)(2,1)S(1)}, u32[]{:S(2)}, u32[]{:S(2)}) %collective-permute-start.22) | collective-permute-done | bytes 200736 | tf_op jit(solution)/shard_map/ppermute | solution.py:28
  190.5 11.1 %collective-permute-done.36 = bf16[2,64,2304]{2,1,0:T(8,128)(2,1)S(1)} collective-permute-done((bf16[2,64,2304]{2,1,0:T(8,128)(2,1)S(1)}, bf16[2,64,2304]{2,1,0:T(8,128)(2,1)S(1)}, u32[]{:S(2)}, u32[]{:S(2)}) %collective-permute-start.36) | collective-permute-done | bytes 589856 | tf_op jit(solution)/shard_map/ppermute | solution.py:38
  207.2 9.1 %collective-permute-done.35 = bf16[2,64,2304]{2,1,0:T(8,128)(2,1)S(1)} collective-permute-done((bf16[2,64,2304]{2,1,0:T(8,128)(2,1)S(1)}, bf16[2,64,2304]{2,1,0:T(8,128)(2,1)S(1)}, u32[]{:S(2)}, u32[]{:S(2)}) %collective-permute-start.35) | collective-permute-done | bytes 589856 | tf_op jit(solution)/shard_map/ppermute | solution.py:38
  218.3 4.5 %collective-permute-start.38 = (bf16[2,64,1152]{2,1,0:T(8,128)(2,1)S(1)}, bf16[2,64,1152]{2,1,0:T(8,128)(2,1)S(1)}, u32[]{:S(2)}, u32[]{:S(2)}) collective-permute-start(bf16[2,64,1152]{2,1,0:T(8,128)(2,1)S(1)} %add_convert_fusion.6), channel_id=1, source_target_pairs={{0,2},{1,3},{2,0},{3,1},{4,6},{5,7},{6,4},{7,5},{8,10},{9,11},{10,... | collective-permute-start | bytes 884744 | tf_op jit(solution)/shard_map/ppermute | solution.py:28
  223.6 11.4 %collective-permute-done.38 = bf16[2,64,1152]{2,1,0:T(8,128)(2,1)S(1)} collective-permute-done((bf16[2,64,1152]{2,1,0:T(8,128)(2,1)S(1)}, bf16[2,64,1152]{2,1,0:T(8,128)(2,1)S(1)}, u32[]{:S(2)}, u32[]{:S(2)}) %collective-permute-start.38) | collective-permute-done | bytes 294944 | tf_op jit(solution)/shard_map/ppermute | solution.py:28
  238.3 8.1 %collective-permute-done.39 = bf16[64,1152]{1,0:T(8,128)(2,1)S(1)} collective-permute-done((bf16[64,1152]{1,0:T(8,128)(2,1)S(1)}, bf16[64,1152]{1,0:T(8,128)(2,1)S(1)}, u32[]{:S(2)}, u32[]{:S(2)}) %collective-permute-start.39) | collective-permute-done | bytes 147488 | tf_op jit(solution)/shard_map/ppermute | solution.py:28
  248.4 19.5 %collective-permute-start.42 = (bf16[64,2304]{1,0:T(8,128)(2,1)S(1)}, bf16[64,2304]{1,0:T(8,128)(2,1)S(1)}, u32[]{:S(2)}, u32[]{:S(2)}) collective-permute-start(bf16[64,2304]{1,0:T(8,128)(2,1)S(1)} %maximum_select_fusion.9), channel_id=1, source_target_pairs={{0,16},{1,17},{2,18},{3,19},{4,20},{5,21},{6,22},{7,23},{8,24},{9,... | collective-permute-start | bytes 884744 | tf_op jit(solution)/shard_map/ppermute | solution.py:38
  268.7 5.4 %collective-permute-start.41 = (bf16[64,2304]{1,0:T(8,128)(2,1)S(1)}, bf16[64,2304]{1,0:T(8,128)(2,1)S(1)}, u32[]{:S(2)}, u32[]{:S(2)}) collective-permute-start(bf16[64,2304]{1,0:T(8,128)(2,1)S(1)} %collective-permute-done.40), channel_id=1, source_target_pairs={{0,16},{1,17},{2,18},{3,19},{4,20},{5,21},{6,22},{7,23},{8,24},{9,... | collective-permute-start | bytes 884744 | tf_op jit(solution)/shard_map/ppermute | solution.py:38
  274.2 4.0 %back_half.6 = (f32[224,896]{1,0:T(8,128)S(1)}, f32[224,896]{1,0:T(8,128)S(1)}) custom-call(s32[3]{0:T(128)S(1)} %pad_add_fusion.8.half_ref, bf16[224,2304]{1,0:T(8,128)(2,1)S(1)} %pad_maximum_fusion.3.x_ref, bf16[4608,1792]{1,0:T(8,128)(2,1)} %bitcast.117), custom_call_target="tpu_custom_call" | custom-call | flops 1849688064 | bytes 8257536 | tf_op jit(solution)/shard_map/back_half/pallas_call | solution.py:128
  280.5 4.0 %back_half.7 = (bf16[224,896]{1,0:T(8,128)(2,1)S(1)}, f32[224,896]{1,0:T(8,128)S(1)}) custom-call(s32[3]{0:T(128)S(1)} %pad_add_fusion.9.half_ref, bf16[224,2304]{1,0:T(8,128)(2,1)S(1)} %pad_maximum_fusion.2.x_ref, bf16[4608,1792]{1,0:T(8,128)(2,1)} %bitcast.118, f32[224,896]{1,0:T(8,128)S(1)} %get-tuple-element.41.refs_0_, ...), custom_call_target="tpu_custom_call" | custom-call | flops 1849688064 | bytes 8257536 | tf_op jit(solution)/shard_map/back_half/pallas_call | solution.py:128
  289.2 13.5 %collective-permute-done.44 = bf16[112,896]{1,0:T(8,128)(2,1)S(1)} collective-permute-done((bf16[112,896]{1,0:T(8,128)(2,1)S(1)}, bf16[112,896]{1,0:T(8,128)(2,1)S(1)}, u32[]{:S(2)}, u32[]{:S(2)}) %collective-permute-start.44) | collective-permute-done | bytes 200736 | tf_op jit(solution)/shard_map/ppermute | solution.py:38
  310.9 6.2 %collective-permute-done.48 = bf16[112,896]{1,0:T(8,128)(2,1)S(1)} collective-permute-done((bf16[112,896]{1,0:T(8,128)(2,1)S(1)}, bf16[112,896]{1,0:T(8,128)(2,1)S(1)}, u32[]{:S(2)}, u32[]{:S(2)}) %collective-permute-start.48) | collective-permute-done | bytes 200736 | tf_op jit(solution)/shard_map/ppermute | solution.py:38
  (217 shorter events, 123.8 us)
Async XLA Ops:
  17.9 57.5 %collective-permute-start.11 = (bf16[2,64,2304]{2,1,0:T(8,128)(2,1)}, bf16[2,64,2304]{2,1,0:T(8,128)(2,1)}, u32[]{:S(2)}, u32[]{:S(2)}) collective-permute-start(bf16[2,64,2304]{2,1,0:T(8,128)(2,1)} %get-tuple-element.30), channel_id=1, source_target_pairs={{0,16},{1,17},{2,18},{3,19},{4,20},{5,21},{6,22},{7,23},{8,24},{9,... | collective-permute-start | bytes 1769480 | tf_op jit(solution)/shard_map/ppermute | solution.py:38
  28.9 84.7 %collective-permute-start.10 = (bf16[2,64,2304]{2,1,0:T(8,128)(2,1)S(1)}, bf16[2,64,2304]{2,1,0:T(8,128)(2,1)}, u32[]{:S(2)}, u32[]{:S(2)}) collective-permute-start(bf16[2,64,2304]{2,1,0:T(8,128)(2,1)S(1)} %get-tuple-element.29), channel_id=1, source_target_pairs={{0,16},{1,17},{2,18},{3,19},{4,20},{5,21},{6,22},{7,23},{8,24},{9,... | collective-permute-start | bytes 1769480 | tf_op jit(solution)/shard_map/ppermute | solution.py:38
  34.6 34.3 %collective-permute-start.6 = (bf16[2,80,2304]{2,1,0:T(8,128)(2,1)S(1)}, bf16[2,80,2304]{2,1,0:T(8,128)(2,1)}, u32[]{:S(2)}, u32[]{:S(2)}) collective-permute-start(bf16[2,80,2304]{2,1,0:T(8,128)(2,1)S(1)} %get-tuple-element.28), channel_id=1, source_target_pairs={{0,1},{1,0},{2,3},{3,2},{4,5},{5,4},{6,7},{7,6},{8,9},{9,8},{10,11... | collective-permute-start | bytes 2211848 | tf_op jit(solution)/shard_map/ppermute | solution.py:28
  36.6 39.6 %collective-permute-start.2 = (bf16[2,80,2304]{2,1,0:T(8,128)(2,1)S(1)}, bf16[2,80,2304]{2,1,0:T(8,128)(2,1)}, u32[]{:S(2)}, u32[]{:S(2)}) collective-permute-start(bf16[2,80,2304]{2,1,0:T(8,128)(2,1)S(1)} %get-tuple-element.26), channel_id=1, source_target_pairs={{0,1},{1,0},{2,3},{3,2},{4,5},{5,4},{6,7},{7,6},{8,9},{9,8},{10,11... | collective-permute-start | bytes 2211848 | tf_op jit(solution)/shard_map/ppermute | solution.py:28
  45.3 22.9 %collective-permute-start.1 = (f32[2,224]{1,0:T(2,128)}, f32[2,224]{1,0:T(2,128)}, u32[]{:S(2)}, u32[]{:S(2)}) collective-permute-start(f32[2,224]{1,0:T(2,128)} %fusion.48), channel_id=1, source_target_pairs={{0,2},{1,3},{2,0},{3,1},{4,6},{5,7},{6,4},{7,5},{8,10},{9,11},{10,... | collective-permute-start | bytes 5384 | tf_op jit(solution)/shard_map/ppermute | solution.py:18
  70.0 30.6 %collective-permute-start.7 = (bf16[2,80,1152]{2,1,0:T(8,128)(2,1)S(1)}, bf16[2,80,1152]{2,1,0:T(8,128)(2,1)S(1)}, u32[]{:S(2)}, u32[]{:S(2)}) collective-permute-start(bf16[2,80,1152]{2,1,0:T(8,128)(2,1)S(1)} %add_convert_fusion.4), channel_id=1, source_target_pairs={{0,2},{1,3},{2,0},{3,1},{4,6},{5,7},{6,4},{7,5},{8,10},{9,11},{10,... | collective-permute-start | bytes 1105928 | tf_op jit(solution)/shard_map/ppermute | solution.py:28
  75.5 38.1 %collective-permute-start.12 = (bf16[2,64,2304]{2,1,0:T(8,128)(2,1)}, bf16[2,64,2304]{2,1,0:T(8,128)(2,1)S(1)}, u32[]{:S(2)}, u32[]{:S(2)}) collective-permute-start(bf16[2,64,2304]{2,1,0:T(8,128)(2,1)} %collective-permute-done.11), channel_id=1, source_target_pairs={{16,17},{17,16},{18,19},{19,18},{20,21},{21,20},{22,23},{23,22},{2... | collective-permute-start | bytes 1769480 | tf_op jit(solution)/shard_map/ppermute | solution.py:28
  77.3 35.2 %collective-permute-start.3 = (bf16[2,80,1152]{2,1,0:T(8,128)(2,1)S(1)}, bf16[2,80,1152]{2,1,0:T(8,128)(2,1)S(1)}, u32[]{:S(2)}, u32[]{:S(2)}) collective-permute-start(bf16[2,80,1152]{2,1,0:T(8,128)(2,1)S(1)} %add_convert_fusion.5), channel_id=1, source_target_pairs={{0,2},{1,3},{2,0},{3,1},{4,6},{5,7},{6,4},{7,5},{8,10},{9,11},{10,... | collective-permute-start | bytes 1105928 | tf_op jit(solution)/shard_map/ppermute | solution.py:28
  102.0 17.4 %collective-permute-start.8 = (bf16[80,1152]{1,0:T(8,128)(2,1)S(1)}, bf16[80,1152]{1,0:T(8,128)(2,1)S(1)}, u32[]{:S(2)}, u32[]{:S(2)}) collective-permute-start(bf16[80,1152]{1,0:T(8,128)(2,1)S(1)} %fusion.20), channel_id=1, source_target_pairs={{0,2},{1,3},{2,0},{3,1},{4,6},{5,7},{6,4},{7,5},{8,10},{9,11},{10,... | collective-permute-start | bytes 552968 | tf_op jit(solution)/shard_map/ppermute | solution.py:28
  119.5 22.0 %collective-permute-start.9 = (bf16[80,2304]{1,0:T(8,128)(2,1)S(1)}, bf16[80,2304]{1,0:T(8,128)(2,1)S(1)}, u32[]{:S(2)}, u32[]{:S(2)}) collective-permute-start(bf16[80,2304]{1,0:T(8,128)(2,1)S(1)} %maximum_select_fusion.5), channel_id=1, source_target_pairs={{0,1},{1,0},{2,3},{3,2},{4,5},{5,4},{6,7},{7,6},{8,9},{9,8},{10,11... | collective-permute-start | bytes 1105928 | tf_op jit(solution)/shard_map/ppermute | solution.py:28
  125.9 15.7 %collective-permute-start.5 = (bf16[80,2304]{1,0:T(8,128)(2,1)S(1)}, bf16[80,2304]{1,0:T(8,128)(2,1)S(1)}, u32[]{:S(2)}, u32[]{:S(2)}) collective-permute-start(bf16[80,2304]{1,0:T(8,128)(2,1)S(1)} %maximum_select_fusion.4), channel_id=1, source_target_pairs={{0,1},{1,0},{2,3},{3,2},{4,5},{5,4},{6,7},{7,6},{8,9},{9,8},{10,11... | collective-permute-start | bytes 1105928 | tf_op jit(solution)/shard_map/ppermute | solution.py:28
  127.8 13.7 %collective-permute-start.16 = (bf16[64,2304]{1,0:T(8,128)(2,1)S(1)}, bf16[64,2304]{1,0:T(8,128)(2,1)S(1)}, u32[]{:S(2)}, u32[]{:S(2)}) collective-permute-start(bf16[64,2304]{1,0:T(8,128)(2,1)S(1)} %collective-permute-done.15), channel_id=1, source_target_pairs={{16,0},{17,1},{18,2},{19,3},{20,4},{21,5},{22,6},{23,7},{24,8},{25... | collective-permute-start | bytes 884744 | tf_op jit(solution)/shard_map/ppermute | solution.py:38
  178.8 22.8 %collective-permute-start.36 = (bf16[2,64,2304]{2,1,0:T(8,128)(2,1)S(1)}, bf16[2,64,2304]{2,1,0:T(8,128)(2,1)S(1)}, u32[]{:S(2)}, u32[]{:S(2)}) collective-permute-start(bf16[2,64,2304]{2,1,0:T(8,128)(2,1)S(1)} %get-tuple-element.40), channel_id=1, source_target_pairs={{16,0},{17,1},{18,2},{19,3},{20,4},{21,5},{22,6},{23,7},{24,8},{25... | collective-permute-start | bytes 1769480 | tf_op jit(solution)/shard_map/ppermute | solution.py:38
  187.5 28.8 %collective-permute-start.35 = (bf16[2,64,2304]{2,1,0:T(8,128)(2,1)S(1)}, bf16[2,64,2304]{2,1,0:T(8,128)(2,1)S(1)}, u32[]{:S(2)}, u32[]{:S(2)}) collective-permute-start(bf16[2,64,2304]{2,1,0:T(8,128)(2,1)S(1)} %get-tuple-element.39), channel_id=1, source_target_pairs={{16,0},{17,1},{18,2},{19,3},{20,4},{21,5},{22,6},{23,7},{24,8},{25... | collective-permute-start | bytes 1769480 | tf_op jit(solution)/shard_map/ppermute | solution.py:38
  188.8 16.4 %collective-permute-start.27 = (bf16[2,80,2304]{2,1,0:T(8,128)(2,1)S(1)}, bf16[2,80,2304]{2,1,0:T(8,128)(2,1)S(1)}, u32[]{:S(2)}, u32[]{:S(2)}) collective-permute-start(bf16[2,80,2304]{2,1,0:T(8,128)(2,1)S(1)} %get-tuple-element.36), channel_id=1, source_target_pairs={{16,17},{17,16},{18,19},{19,18},{20,21},{21,20},{22,23},{23,22},{2... | collective-permute-start | bytes 2211848 | tf_op jit(solution)/shard_map/ppermute | solution.py:28
  189.7 16.3 %collective-permute-start.32 = (bf16[2,80,1152]{2,1,0:T(8,128)(2,1)S(1)}, bf16[2,80,1152]{2,1,0:T(8,128)(2,1)S(1)}, u32[]{:S(2)}, u32[]{:S(2)}) collective-permute-start(bf16[2,80,1152]{2,1,0:T(8,128)(2,1)S(1)} %add_convert_fusion.2), channel_id=1, source_target_pairs={{16,18},{17,19},{18,16},{19,17},{20,22},{21,23},{22,20},{23,21},{2... | collective-permute-start | bytes 1105928 | tf_op jit(solution)/shard_map/ppermute | solution.py:28
  201.6 16.7 %collective-permute-start.37 = (bf16[2,64,2304]{2,1,0:T(8,128)(2,1)S(1)}, bf16[2,64,2304]{2,1,0:T(8,128)(2,1)S(1)}, u32[]{:S(2)}, u32[]{:S(2)}) collective-permute-start(bf16[2,64,2304]{2,1,0:T(8,128)(2,1)S(1)} %collective-permute-done.36), channel_id=1, source_target_pairs={{0,1},{1,0},{2,3},{3,2},{4,5},{5,4},{6,7},{7,6},{8,9},{9,8},{10,11... | collective-permute-start | bytes 1769480 | tf_op jit(solution)/shard_map/ppermute | solution.py:28
  206.3 31.1 %collective-permute-start.33 = (bf16[80,1152]{1,0:T(8,128)(2,1)S(1)}, bf16[80,1152]{1,0:T(8,128)(2,1)S(1)}, u32[]{:S(2)}, u32[]{:S(2)}) collective-permute-start(bf16[80,1152]{1,0:T(8,128)(2,1)S(1)} %fusion.12), channel_id=1, source_target_pairs={{16,18},{17,19},{18,16},{19,17},{20,22},{21,23},{22,20},{23,21},{2... | collective-permute-start | bytes 552968 | tf_op jit(solution)/shard_map/ppermute | solution.py:28
  218.3 16.7 %collective-permute-start.38 = (bf16[2,64,1152]{2,1,0:T(8,128)(2,1)S(1)}, bf16[2,64,1152]{2,1,0:T(8,128)(2,1)S(1)}, u32[]{:S(2)}, u32[]{:S(2)}) collective-permute-start(bf16[2,64,1152]{2,1,0:T(8,128)(2,1)S(1)} %add_convert_fusion.6), channel_id=1, source_target_pairs={{0,2},{1,3},{2,0},{3,1},{4,6},{5,7},{6,4},{7,5},{8,10},{9,11},{10,... | collective-permute-start | bytes 884744 | tf_op jit(solution)/shard_map/ppermute | solution.py:28
  223.0 44.9 %collective-permute-start.29 = (bf16[80,1152]{1,0:T(8,128)(2,1)S(1)}, bf16[80,1152]{1,0:T(8,128)(2,1)S(1)}, u32[]{:S(2)}, u32[]{:S(2)}) collective-permute-start(bf16[80,1152]{1,0:T(8,128)(2,1)S(1)} %fusion.16), channel_id=1, source_target_pairs={{16,18},{17,19},{18,16},{19,17},{20,22},{21,23},{22,20},{23,21},{2... | collective-permute-start | bytes 552968 | tf_op jit(solution)/shard_map/ppermute | solution.py:28
  237.6 40.6 %collective-permute-start.34 = (bf16[80,2304]{1,0:T(8,128)(2,1)S(1)}, bf16[80,2304]{1,0:T(8,128)(2,1)S(1)}, u32[]{:S(2)}, u32[]{:S(2)}) collective-permute-start(bf16[80,2304]{1,0:T(8,128)(2,1)S(1)} %maximum_select_fusion.7), channel_id=1, source_target_pairs={{16,17},{17,16},{18,19},{19,18},{20,21},{21,20},{22,23},{23,22},{2... | collective-permute-start | bytes 1105928 | tf_op jit(solution)/shard_map/ppermute | solution.py:28
  246.5 22.2 %collective-permute-start.40 = (bf16[64,2304]{1,0:T(8,128)(2,1)S(1)}, bf16[64,2304]{1,0:T(8,128)(2,1)S(1)}, u32[]{:S(2)}, u32[]{:S(2)}) collective-permute-start(bf16[64,2304]{1,0:T(8,128)(2,1)S(1)} %maximum_select_fusion.9), channel_id=1, source_target_pairs={{0,1},{1,0},{2,3},{3,2},{4,5},{5,4},{6,7},{7,6},{8,9},{9,8},{10,11... | collective-permute-start | bytes 884744 | tf_op jit(solution)/shard_map/ppermute | solution.py:28
  248.4 25.7 %collective-permute-start.42 = (bf16[64,2304]{1,0:T(8,128)(2,1)S(1)}, bf16[64,2304]{1,0:T(8,128)(2,1)S(1)}, u32[]{:S(2)}, u32[]{:S(2)}) collective-permute-start(bf16[64,2304]{1,0:T(8,128)(2,1)S(1)} %maximum_select_fusion.9), channel_id=1, source_target_pairs={{0,16},{1,17},{2,18},{3,19},{4,20},{5,21},{6,22},{7,23},{8,24},{9,... | collective-permute-start | bytes 884744 | tf_op jit(solution)/shard_map/ppermute | solution.py:38
  287.4 15.3 %collective-permute-start.44 = (bf16[112,896]{1,0:T(8,128)(2,1)S(1)}, bf16[112,896]{1,0:T(8,128)(2,1)S(1)}, u32[]{:S(2)}, u32[]{:S(2)}) collective-permute-start(bf16[112,896]{1,0:T(8,128)(2,1)S(1)} %slice.202), channel_id=1, source_target_pairs={{16,0},{17,1},{18,2},{19,3},{20,4},{21,5},{22,6},{23,7},{24,8},{25... | collective-permute-start | bytes 602120 | tf_op jit(solution)/shard_map/ppermute | solution.py:38
  (39 other events, 281.5 us)
